TPU v7x, 8 devices: a whole 2x2x1 slice. The times are simulated.
8 devices in a mesh: rep: 2 (over y, z), dp: 4 (over x, core).
Axes of the slice: x: 2, y: 2, z: 1, core: 2. Of those that a mesh axis runs over, the one named last changes fastest.
Arguments:
- x: bfloat16 [8, 2048, 1280], P(('rep', 'dp')), parts along dimension 0
- dy: bfloat16 [8, 2048, 1280], P(('rep', 'dp')), parts along dimension 0
- w_gate: bfloat16 [2, 1280, 4096], P(None, 'dp')
- w_up: bfloat16 [2, 1280, 4096], P(None, 'dp')
- w_down: bfloat16 [2, 4096, 1280], P(None, 'dp')
- m_w_gate: float32 [2, 1280, 4096], P(None, 'dp')
- m_w_up: float32 [2, 1280, 4096], P(None, 'dp')
- m_w_down: float32 [2, 4096, 1280], P(None, 'dp')
- v_w_gate: float32 [2, 1280, 4096], P(None, 'dp')
- v_w_up: float32 [2, 1280, 4096], P(None, 'dp')
- v_w_down: float32 [2, 4096, 1280], P(None, 'dp')
Outputs:
- output 1: bfloat16 [4, 1280, 4096], P('rep', 'dp'), parts along dimension 0
- output 2: bfloat16 [4, 1280, 4096], P('rep', 'dp'), parts along dimension 0
- output 3: bfloat16 [4, 4096, 1280], P('rep', 'dp'), parts along dimension 0
- output 4: float32 [4, 1280, 4096], P('rep', 'dp'), parts along dimension 0
- output 5: float32 [4, 1280, 4096], P('rep', 'dp'), parts along dimension 0
- output 6: float32 [4, 4096, 1280], P('rep', 'dp'), parts along dimension 0
- output 7: float32 [4, 1280, 4096], P('rep', 'dp'), parts along dimension 0
- output 8: float32 [4, 1280, 4096], P('rep', 'dp'), parts along dimension 0
- output 9: float32 [4, 4096, 1280], P('rep', 'dp'), parts along dimension 0
There are 2 independent parts. A program takes and returns all parts, laid end to end along the dimension named above; an argument that names none is the same for every part.
All inputs are finite; a program needn't handle non-finite values.
Results may differ from a plain program's by a relative error of at most 0.022.
Values are sent between devices in bfloat16 or wider.
A program may use at most 2 GiB of HBM per device.

v0:
```python
import jax
import jax.numpy as jnp
from jax import lax
from jax.sharding import PartitionSpec as P

NAMES = ("w_gate", "w_up", "w_down")


def matmul(a, w):
    return jnp.dot(a, w, preferred_element_type=jnp.float32).astype(jnp.bfloat16)


def normed(h):
    wide = h.astype(jnp.float32)
    scale = lax.rsqrt(jnp.mean(wide**2, -1, keepdims=True) + 1e-6)
    return (wide * scale).astype(jnp.bfloat16)


def layer(h, w):
    a = normed(h)
    gate = jnp.dot(a, w["w_gate"], preferred_element_type=jnp.float32)
    up = jnp.dot(a, w["w_up"], preferred_element_type=jnp.float32)
    return h + matmul((jax.nn.silu(gate) * up).astype(jnp.bfloat16), w["w_down"])


def adamw(w, m, v, g):
    m = 0.9 * m + 0.1 * g
    v = 0.95 * v + 0.05 * g * g
    step = m * lax.rsqrt(v + 1e-8) + 0.1 * w
    return (w - 0.02 * step).astype(jnp.bfloat16), m, v


def solution(mesh):
    def fetched(weights, number):
        return {name: lax.all_gather(w[number], "dp", axis=0, tiled=True) for name, w in zip(NAMES, weights, strict=True)}

    def step(x, dy, *arrays):
        weights, m, v = (arrays[i : i + 3] for i in (0, 3, 6))
        layers = weights[0].shape[0]
        h, kept = x[0], []
        for number in range(layers):
            kept.append(h)
            h = layer(h, fetched(weights, number))
        by_h, mine = dy[0], [None] * layers
        for number in reversed(range(layers)):
            _, back = jax.vjp(lambda w, h: layer(h, w), fetched(weights, number), kept[number])
            by_w, by_h = back(by_h)
            mine[number] = [lax.psum_scatter(by_w[name], "dp", scatter_dimension=0, tiled=True) for name in NAMES]
        gradients = [jnp.stack([mine[number][i] for number in range(layers)]).astype(jnp.float32) for i in range(3)]
        new = [adamw(w.astype(jnp.float32), m, v, g) for w, m, v, g in zip(weights, m, v, gradients, strict=True)]
        return tuple(one[which] for which in range(3) for one in new)

    states, cut = P(("rep", "dp"), None, None), P(None, "dp", None)
    return jax.shard_map(
        step,
        mesh=mesh,
        in_specs=(states, states) + (cut,) * 9,
        out_specs=(P("rep", "dp", None),) * 9,
        check_vma=False,
    )
```

profile of v0, /device:TPU:0, one launch (start us, length us, event | category | flops | bytes accessed | tf_op | source)
XLA Modules:
  0.0 1129.7 jit_solution(17468959340203498735)
XLA Ops:
  44.8 38.8 %all-gather.13.cloned.1.call-done = bf16[1,1280,4096]{2,1,0:T(8,128)(2,1)} async-done(((bf16[1,320,4096]{2,1,0:T(8,128)(2,1)}), bf16[1,1280,4096]{2,1,0:T(8,128)(2,1)}) %all-gather.13.cloned.1.call-update) | async-done | bytes 10485776 | tf_op jit(solution)/shard_map/all_gather | solution.py:35
  83.6 29.3 %fusion.56 = f32[2048,4096]{1,0:T(8,128)} fusion(bf16[1,1280,4096]{2,1,0:T(8,128)(2,1)} %all-gather.13.cloned.1.call-done, bf16[1,2048,1280]{1,2,0:T(8,128)(2,1)} %copy.20, f32[2048]{0:T(1024)S(1)} %add_rsqrt_fusion), kind=kOutput, calls=%fused_computation.86 | convolution fusion | flops 21482700800 | bytes 49291264 | tf_op jit(solution)/shard_map/dot_general | solution.py:21
  112.9 40.7 %all-gather.15.cloned.1.call-done = bf16[1,1280,4096]{2,1,0:T(8,128)(2,1)} async-done(((bf16[1,320,4096]{2,1,0:T(8,128)(2,1)}), bf16[1,1280,4096]{2,1,0:T(8,128)(2,1)}) %all-gather.15.cloned.1.call-update) | async-done | bytes 10485776 | tf_op jit(solution)/shard_map/all_gather | solution.py:35
  153.6 41.5 %multiply_convert_fusion.1 = (bf16[2048,4096]{1,0:T(8,128)(2,1)}, f32[2048,4096]{1,0:T(8,128)}) fusion(f32[2048,4096]{1,0:T(8,128)} %fusion.56, bf16[1,1280,4096]{2,1,0:T(8,128)(2,1)} %all-gather.15.cloned.1.call-done, bf16[1,2048,1280]{1,2,0:T(8,128)(2,1)} %copy.20, f32[2048]{0:T(1024)S(1)} %add_rsqrt_fusion), kind=kOutput, calls=%fused_computation.17 | convolution fusion | flops 21533032448 | bytes 99622912 | tf_op jit(solution)/shard_map/dot_general | solution.py:22
  195.0 28.5 %all-gather.17.cloned.1.call-done = bf16[1,4096,1280]{2,1,0:T(8,128)(2,1)} async-done(((bf16[1,1024,1280]{2,1,0:T(8,128)(2,1)}), bf16[1,4096,1280]{2,1,0:T(8,128)(2,1)}) %all-gather.17.cloned.1.call-update) | async-done | bytes 10485776 | tf_op jit(solution)/shard_map/all_gather | solution.py:35
  223.5 30.5 %fusion.40 = (f32[2048]{0:T(1024)S(1)}, bf16[2048,1280]{0,1:T(8,128)(2,1)}) fusion(bf16[2048,4096]{1,0:T(8,128)(2,1)} %get-tuple-element.24, bf16[1,4096,1280]{2,1,0:T(8,128)(2,1)} %all-gather.17.cloned.1.call-done, bf16[1,2048,1280]{1,2,0:T(8,128)(2,1)} %copy.20), kind=kOutput, calls=%fused_computation.70 | convolution fusion | flops 21487941632 | bytes 37756928 | tf_op jit(solution)/shard_map/dot_general | solution.py:10
  254.1 39.3 %all-gather.21.cloned.1.call-done = bf16[1,4096,1280]{2,1,0:T(8,128)(2,1)} async-done(((bf16[1,1024,1280]{2,1,0:T(8,128)(2,1)}), bf16[1,4096,1280]{2,1,0:T(8,128)(2,1)}) %all-gather.21.cloned.1.call-update) | async-done | bytes 10485776 | tf_op jit(solution)/shard_map/all_gather | solution.py:35
  293.4 28.9 %convolution_convert_fusion.3 = bf16[2048,4096]{1,0:T(8,128)(2,1)} fusion(bf16[1,4096,1280]{2,1,0:T(8,128)(2,1)} %all-gather.21.cloned.1.call-done, bf16[1,2048,1280]{2,1,0:T(8,128)(2,1)} %param.12), kind=kOutput, calls=%fused_computation.38 | convolution fusion | flops 21483225088 | bytes 32505856 | tf_op jit(solution)/shard_map/transpose(jvp())/dot_general | solution.py:10
  322.3 40.9 %all-gather.23.cloned.1.call-done = bf16[1,1280,4096]{2,1,0:T(8,128)(2,1)} async-done(((bf16[1,320,4096]{2,1,0:T(8,128)(2,1)}), bf16[1,1280,4096]{2,1,0:T(8,128)(2,1)}) %all-gather.23.cloned.1.call-update) | async-done | bytes 10485776 | tf_op jit(solution)/shard_map/all_gather | solution.py:35
  363.2 29.4 %fusion.43 = f32[2048,4096]{1,0:T(8,128)} fusion(bf16[1,1280,4096]{2,1,0:T(8,128)(2,1)} %all-gather.23.cloned.1.call-done, bf16[2048,1280]{0,1:T(8,128)(2,1)} %get-tuple-element.27, f32[2048]{0:T(1024)S(1)} %fusion.85), kind=kOutput, calls=%fused_computation.73 | convolution fusion | flops 21482700800 | bytes 49291264 | tf_op jit(solution)/shard_map/jvp()/dot_general | solution.py:22
  392.6 40.4 %all-gather.19.cloned.1.call-done = bf16[1,1280,4096]{2,1,0:T(8,128)(2,1)} async-done(((bf16[1,320,4096]{2,1,0:T(8,128)(2,1)}), bf16[1,1280,4096]{2,1,0:T(8,128)(2,1)}) %all-gather.19.cloned.1.call-update) | async-done | bytes 10485776 | tf_op jit(solution)/shard_map/all_gather | solution.py:35
  433.0 49.9 %fusion.2 = (bf16[2048,4096]{1,0:T(8,128)(2,1)}, f32[2048,4096]{1,0:T(8,128)}) fusion(f32[2048,4096]{1,0:T(8,128)} %fusion.43, bf16[2048,4096]{1,0:T(8,128)(2,1)} %convolution_convert_fusion.3, bf16[1,1280,4096]{2,1,0:T(8,128)(2,1)} %all-gather.19.cloned.1.call-done, bf16[2048,1280]{0,1:T(8,128)(2,1)} %get-tuple-element.27, f32[2048]{0:T(1024)S(1)} %fusion.85), kind=kOutput, calls=%fused_computation.8 | convolution fusion | flops 21583364096 | bytes 116400128 | tf_op jit(solution)/shard_map/jvp()/dot_general | solution.py:21
  482.9 29.1 %fusion.64 = bf16[2048,1280]{0,1:T(8,128)(2,1)} fusion(bf16[2048,4096]{1,0:T(8,128)(2,1)} %get-tuple-element.28, bf16[1,1280,4096]{2,1,0:T(8,128)(2,1)} %all-gather.19.cloned.1.call-done), kind=kOutput, calls=%fused_computation.90 | convolution fusion | flops 21474836480 | bytes 32505856 | tf_op jit(solution)/shard_map/transpose(jvp())/dot_general | solution.py:21
  512.1 37.4 %fusion.42 = (f32[2048]{0:T(1024)S(1)}, bf16[2048,1280]{0,1:T(8,128)(2,1)}) fusion(bf16[2048,1280]{0,1:T(8,128)(2,1)} %get-tuple-element.27, bf16[2048,1280]{0,1:T(8,128)(2,1)} %fusion.64, bf16[1,1280,4096]{2,1,0:T(8,128)(2,1)} %all-gather.23.cloned.1.call-done, bf16[2048,4096]{1,0:T(8,128)(2,1)} %convolution_convert_fusion.3, ...), kind=kOutput, calls=%fused_computation.72 | convolution fusion | flops 21540894720 | bytes 76554240 | tf_op jit(solution)/shard_map/transpose(jvp())/dot_general | solution.py:22
  561.9 29.1 %convolution_convert_fusion.2 = bf16[2048,4096]{1,0:T(8,128)(2,1)} fusion(bf16[2048,1280]{0,1:T(8,128)(2,1)} %fusion.74, bf16[1,4096,1280]{2,1,0:T(8,128)(2,1)} %all-gather.17.cloned.1.call-done), kind=kOutput, calls=%fused_computation.37 | convolution fusion | flops 21483225088 | bytes 32505856 | tf_op jit(solution)/shard_map/transpose(jvp())/dot_general | solution.py:10
  591.0 30.9 %fusion.20 = bf16[1280,4096]{1,0:T(8,128)(2,1)} fusion(bf16[2048,4096]{1,0:T(8,128)(2,1)} %convolution_convert_fusion.2, f32[2048,4096]{1,0:T(8,128)} %fusion.56, bf16[1,2048,1280]{1,2,0:T(8,128)(2,1)} %copy.20, f32[2048]{0:T(1024)S(1)} %copy-done.5), kind=kOutput, calls=%fused_computation.35 | convolution fusion | flops 21538275328 | bytes 66068480 | tf_op jit(solution)/shard_map/transpose(jvp())/dot_general | solution.py:22
  621.9 30.7 %fusion.16 = bf16[1280,4096]{1,0:T(8,128)(2,1)} fusion(bf16[2048,4096]{1,0:T(8,128)(2,1)} %convolution_convert_fusion.3, bf16[2048,1280]{0,1:T(8,128)(2,1)} %get-tuple-element.27, f32[2048]{0:T(1024)S(1)} %fusion.85, f32[2048,4096]{1,0:T(8,128)} %get-tuple-element.29), kind=kOutput, calls=%fused_computation.33 | convolution fusion | flops 21538275328 | bytes 66068480 | tf_op jit(solution)/shard_map/transpose(jvp())/dot_general | solution.py:22
  652.7 35.3 %fusion.15 = bf16[4096,1280]{1,0:T(8,128)(2,1)} fusion(f32[2048,4096]{1,0:T(8,128)} %fusion.43, bf16[1,2048,1280]{2,1,0:T(8,128)(2,1)} %param.12, f32[2048,4096]{1,0:T(8,128)} %get-tuple-element.29), kind=kOutput, calls=%fused_computation.32 | convolution fusion | flops 21530411008 | bytes 82837504 | tf_op jit(solution)/shard_map/transpose(jvp())/dot_general | solution.py:10
  688.1 28.0 %convolution_convert_fusion.1 = bf16[4096,1280]{1,0:T(8,128)(2,1)} fusion(bf16[2048,4096]{1,0:T(8,128)(2,1)} %get-tuple-element.24, bf16[2048,1280]{0,1:T(8,128)(2,1)} %fusion.74), kind=kOutput, calls=%fused_computation.36 | convolution fusion | flops 21480079360 | bytes 32505856 | tf_op jit(solution)/shard_map/transpose(jvp())/dot_general | solution.py:10
  716.8 39.9 %fusion.17 = bf16[1280,4096]{1,0:T(8,128)(2,1)} fusion(f32[2048,4096]{1,0:T(8,128)} %fusion.56, f32[2048,4096]{1,0:T(8,128)} %get-tuple-element.25, bf16[2048,4096]{1,0:T(8,128)(2,1)} %convolution_convert_fusion.2, bf16[1,2048,1280]{1,2,0:T(8,128)(2,1)} %copy.20, f32[2048]{0:T(1024)S(1)} %copy-done.6), kind=kOutput, calls=%fused_computation.34 | convolution fusion | flops 21580218368 | bytes 99622912 | tf_op jit(solution)/shard_map/transpose(jvp())/dot_general | solution.py:21
  804.4 57.0 %reduce-scatter.17.cloned.1.call-done = bf16[1024,1280]{1,0:T(8,128)(2,1)} async-done(((bf16[4096,1280]{1,0:T(8,128)(2,1)}), bf16[1024,1280]{1,0:T(8,128)(2,1)}) %reduce-scatter.17.cloned.1.call-update) | async-done | bytes 2621456 | tf_op jit(solution)/shard_map/reduce_scatter | solution.py:48
  861.4 80.3 %reduce-scatter.15.cloned.1.call-done = bf16[1024,1280]{1,0:T(8,128)(2,1)} async-done(((bf16[4096,1280]{1,0:T(8,128)(2,1)}), bf16[1024,1280]{1,0:T(8,128)(2,1)}) %reduce-scatter.15.cloned.1.call-update) | async-done | bytes 2621456 | tf_op jit(solution)/shard_map/reduce_scatter | solution.py:48
  963.4 59.4 %reduce-scatter.7.cloned.1.call-done = bf16[320,4096]{1,0:T(8,128)(2,1)} async-done(((bf16[1280,4096]{1,0:T(8,128)(2,1)}), bf16[320,4096]{1,0:T(8,128)(2,1)}) %reduce-scatter.7.cloned.1.call-update) | async-done | bytes 2621456 | tf_op jit(solution)/shard_map/reduce_scatter | solution.py:48
  1022.8 80.9 %reduce-scatter.9.cloned.1.call-done = bf16[320,4096]{1,0:T(8,128)(2,1)} async-done(((bf16[1280,4096]{1,0:T(8,128)(2,1)}), bf16[320,4096]{1,0:T(8,128)(2,1)}) %reduce-scatter.9.cloned.1.call-update) | async-done | bytes 2621456 | tf_op jit(solution)/shard_map/reduce_scatter | solution.py:48
  (54 shorter events, 139.1 us)
Async XLA Ops:
  7.2 76.4 %all-gather.13.cloned.1.call-start = ((), (), s32[]{:S(2)}) async-start(), calls=%async_computation.12 | async-start | bytes 13107200 | tf_op jit(solution)/shard_map/all_gather | solution.py:35
  12.8 140.8 %all-gather.15.cloned.1.call-start = ((), (), s32[]{:S(2)}) async-start(), calls=%async_computation.13 | async-start | bytes 13107200 | tf_op jit(solution)/shard_map/all_gather | solution.py:35
  18.4 205.2 %all-gather.17.cloned.1.call-start = ((), (), s32[]{:S(2)}) async-start(), calls=%async_computation.14 | async-start | bytes 13107200 | tf_op jit(solution)/shard_map/all_gather | solution.py:35
  23.7 269.7 %all-gather.21.cloned.1.call-start = ((), (), s32[]{:S(2)}) async-start(), calls=%async_computation.16 | async-start | bytes 13107200 | tf_op jit(solution)/shard_map/all_gather | solution.py:35
  24.3 338.9 %all-gather.23.cloned.1.call-start = ((), (), s32[]{:S(2)}) async-start(), calls=%async_computation.17 | async-start | bytes 13107200 | tf_op jit(solution)/shard_map/all_gather | solution.py:35
  24.8 408.2 %all-gather.19.cloned.1.call-start = ((), (), s32[]{:S(2)}) async-start(), calls=%async_computation.15 | async-start | bytes 13107200 | tf_op jit(solution)/shard_map/all_gather | solution.py:35
  25.4 759.9 %reduce-scatter.11.cloned.1.call-start = ((), (), s32[]{:S(2)}) async-start(), calls=%async_computation.8 | async-start | bytes 13107200 | tf_op jit(solution)/shard_map/reduce_scatter | solution.py:48
  36.9 116.6 %copy-start.4 = (f32[2048]{0:T(1024)}, f32[2048]{0:T(1024)S(1)}, u32[]{:S(2)}) copy-start(f32[2048]{0:T(1024)S(1)} %add_rsqrt_fusion) | copy-start | bytes 24580
  254.1 68.2 %copy-start.2 = (f32[2048]{0:T(1024)}, f32[2048]{0:T(1024)S(1)}, u32[]{:S(2)}) copy-start(f32[2048]{0:T(1024)S(1)} %get-tuple-element.26) | copy-start | bytes 24580
  254.1 367.8 %copy-start = (f32[2048]{0:T(1024)}, f32[2048]{0:T(1024)S(1)}, u32[]{:S(2)}) copy-start(f32[2048]{0:T(1024)S(1)} %fusion.85) | copy-start | bytes 24580
  512.1 37.4 %copy-start.3 = (f32[2048]{0:T(1024)S(1)}, f32[2048]{0:T(1024)}, u32[]{:S(2)}) copy-start(f32[2048]{0:T(1024)} %copy-done.2) | copy-start | bytes 24580
  561.9 29.1 %copy-start.5 = (f32[2048]{0:T(1024)S(1)}, f32[2048]{0:T(1024)}, u32[]{:S(2)}) copy-start(f32[2048]{0:T(1024)} %copy-done.4) | copy-start | bytes 24580
  621.9 163.5 %reduce-scatter.13.cloned.1.call-start = ((), (), s32[]{:S(2)}) async-start(), calls=%async_computation.9 | async-start | bytes 13107200 | tf_op jit(solution)/shard_map/reduce_scatter | solution.py:48
  652.6 208.8 %reduce-scatter.17.cloned.1.call-start = ((), (), s32[]{:S(2)}) async-start(), calls=%async_computation.11 | async-start | bytes 13107200 | tf_op jit(solution)/shard_map/reduce_scatter | solution.py:48
  688.1 253.7 %reduce-scatter.15.cloned.1.call-start = ((), (), s32[]{:S(2)}) async-start(), calls=%async_computation.10 | async-start | bytes 13107200 | tf_op jit(solution)/shard_map/reduce_scatter | solution.py:48
  716.1 0.7 copy-start.6
  716.2 306.6 %reduce-scatter.7.cloned.1.call-start = ((), (), s32[]{:S(2)}) async-start(), calls=%async_computation.6 | async-start | bytes 13107200 | tf_op jit(solution)/shard_map/reduce_scatter | solution.py:48
  756.7 0.7 copy-start.1
  756.8 346.9 %reduce-scatter.9.cloned.1.call-start = ((), (), s32[]{:S(2)}) async-start(), calls=%async_computation.7 | async-start | bytes 13107200 | tf_op jit(solution)/shard_map/reduce_scatter | solution.py:48
Sparse Core Ops, SparseCore 0:
  12.9 70.6 all-gather.12
  85.7 67.8 all-gather.14
  155.7 67.8 all-gather.16
  225.5 67.8 all-gather.20
  295.3 67.8 all-gather.22
  365.1 67.8 all-gather.18
  622.0 77.8 reduce-scatter.10
  703.0 77.8 reduce-scatter.12
  783.5 77.8 reduce-scatter.16
  863.8 77.8 reduce-scatter.14
  944.9 77.8 reduce-scatter.6
  1025.7 77.8 reduce-scatter.8
where the time goes:
time: 1140 us; the launch traced here: 1130 us
  waiting for transfers between devices  508 us (45%)
  matrix products  498 us (44%)
  other arithmetic  75.6 us (7%)
  local copies, waits for them, and re-layouts  33.3 us (3%)
  between operations  14.5 us (1%)
    reduce_scatter x6, waiting for transfers between devices, step(): lax.psum_scatter(by_w[name], 'dp', scatter_dimension=0, tiled=True)  278 us
    all_gather x6, waiting for transfers between devices, fetched(): lax.all_gather(w[number], 'dp', axis=0, tiled=True)  229 us
    dot_general x5, matrix products, layer(): gate = jnp.dot(a, w['w_gate'], preferred_element_type=jnp.float32)  176 us
    dot_general x5, matrix products, layer(): up = jnp.dot(a, w['w_up'], preferred_element_type=jnp.float32)  170 us
    dot_general x5, matrix products, matmul(): jnp.dot(a, w, preferred_element_type=jnp.float32).astype(jnp.bfloat16)  152 us
    convert_element_type x3, other arithmetic, adamw(): return ((w - 0.02 * step).astype(jnp.bfloat16), m, v)  59.6 us
  transfers between devices with their start and end apart: 12, of which 10 were waited for; matrix products, arithmetic and copies ran while one was open for 35% of the time, Pallas kernels for 0%

commit v1 on v0

v1 whole, which is shorter than its diff:
```python
import functools
import jax, jax.numpy as jnp
from jax import lax
from jax.experimental import pallas as pl
from jax.experimental.pallas import tpu as pltpu
from jax.sharding import PartitionSpec as P
WIDE = jnp.float32
NARROW = jnp.bfloat16
MIB = 2**20
MESH = pl.DeviceIdType.MESH
WHOLE = pl.BlockSpec(memory_space=pl.ANY)

CHUNKS, TILES, PIECES, AHEAD = 8, 2, 4, 8

def forward_kernel(number, first, *refs):
    if first:
        (h_ref, wg, wu, wd, act_ref, gate_ref, up_ref, a_ref, full_gu, full_d), scratch = refs[:10], refs[10:]
    else:
        (h_ref, actp_ref, wdp_ref, wg, wu, wd, act_ref, gate_ref, up_ref, a_ref, h_out, full_gu, full_d), scratch = refs[:13], refs[13:]
    (slots, own_gu, own_d, own_sem, load_sem, o_send, o_recv, x_send, x_recv, xd_send, xd_recv,
     y_send, y_recv, sx_send, sx_recv, sy_send, sy_recv) = scratch
    n = pl.program_id(0)
    rep, dp = lax.axis_index("rep"), lax.axis_index("dp")
    far, beside = (dp + 2) % 4, dp + 1 - 2 * (dp % 2)
    over_x, over_y, over_core = (rep, far), (1 - rep, dp), (rep, beside)
    rows_gu, rows_d = own_gu.shape[1], own_d.shape[0]
    cols = slots.shape[-1]
    half_gu, half_d = rows_gu // 2, rows_d // 2
    piece = half_d // PIECES

    def chunk(k):
        return pl.ds(pl.multiple_of(k * cols, cols), cols)

    def part_gu(start, size, k):
        return full_gu.at[:, pl.ds(pl.multiple_of(start, half_gu), size), chunk(k)]

    def part_d(start, size):
        return full_d.at[pl.ds(pl.multiple_of(start, piece), size), :]

    def remote(src, dst, send, recv, device):
        return pltpu.make_async_remote_copy(src, dst, send, recv, device_id=device, device_id_type=MESH)

    def own_copies(to):
        out = []
        for i, w in enumerate((wg, wu)):
            start = pl.multiple_of(to * rows_gu, half_gu)
            out.append(remote(w.at[number], full_gu.at[i, pl.ds(start, rows_gu), :], o_send.at[i], o_recv.at[i], over_core))
        out.append(remote(wd.at[number], part_d(to * rows_d, rows_d), o_send.at[2], o_recv.at[2], over_core))
        return out

    def x_copies(owner, k):
        out = []
        for i, w in enumerate((wg, wu)):
            start = pl.multiple_of(rep * half_gu, half_gu)
            dst = full_gu.at[i, pl.ds(pl.multiple_of(owner * rows_gu + rep * half_gu, half_gu), half_gu), chunk(k)]
            out.append(remote(w.at[number, pl.ds(start, half_gu), chunk(k)], dst, x_send.at[i, k], x_recv.at[i, k], over_x))
        return out

    def xd_copy(owner, k):
        start = pl.multiple_of(rep * half_d + k * piece, piece)
        dst = part_d(owner * rows_d + rep * half_d + k * piece, piece)
        return remote(wd.at[number, pl.ds(start, piece), :], dst, xd_send.at[k], xd_recv.at[k], over_x)

    def relay(owner, half, k, send, recv, device):
        gu = part_gu(owner * rows_gu + half * half_gu, half_gu, k)
        return remote(gu, gu, send.at[k], recv.at[k], device)

    def relay_d(owner, half, k, send, recv, device):
        d = part_d(owner * rows_d + half * half_d + k * piece, piece)
        return remote(d, d, send.at[CHUNKS + k], recv.at[CHUNKS + k], device)

    def relays(k, make):
        @pl.when((k >= 0) & (k < CHUNKS))
        def _():
            make(k, False)

        @pl.when((k >= CHUNKS) & (k < CHUNKS + PIECES))
        def _():
            make(k - CHUNKS, True)

    def own_in():
        return [pltpu.make_async_copy(wg.at[number], own_gu.at[0], own_sem.at[0]),
                pltpu.make_async_copy(wu.at[number], own_gu.at[1], own_sem.at[1]),
                pltpu.make_async_copy(wd.at[number], own_d, own_sem.at[2])]

    def own_out():
        start = pl.multiple_of(dp * rows_gu, half_gu)
        return [pltpu.make_async_copy(own_gu.at[0], full_gu.at[0, pl.ds(start, rows_gu), :], own_sem.at[3]),
                pltpu.make_async_copy(own_gu.at[1], full_gu.at[1, pl.ds(start, rows_gu), :], own_sem.at[4]),
                pltpu.make_async_copy(own_d, part_d(dp * rows_d, rows_d), own_sem.at[5])]

    def load(k):
        return pltpu.make_async_copy(full_gu.at[:, :, chunk(k)], slots.at[k % 2], load_sem.at[k % 2])

    @pl.when(n == 0)
    def _():
        barrier = pltpu.get_barrier_semaphore()
        for device in (over_x, over_y, over_core):
            pl.semaphore_signal(barrier, inc=1, device_id=device, device_id_type=MESH)
        pl.semaphore_wait(barrier, 3)
        for copy in own_in():
            copy.start()
        for k in range(CHUNKS):
            for copy in x_copies(dp, k):
                copy.start()
        for k in range(PIECES):
            xd_copy(dp, k).start()
        for copy in own_copies(dp):
            copy.start()
        if first:
            wide = h_ref[...].astype(WIDE)
            scale = lax.rsqrt(jnp.mean(wide * wide, -1, keepdims=True) + 1e-6)
            a_ref[...] = (wide * scale).astype(NARROW)

    @pl.when(n == 1)
    def _():
        for into, out in zip(own_in(), own_out()):
            into.wait()
            out.start()

    @pl.when(n == 5)
    def _():
        for out in own_out():
            out.wait()
        for copy in own_copies(beside):
            copy.wait_recv()

    odd = n % 2 == 1

    @pl.when(odd)
    def _():
        def forward_x(k, down):
            if down:
                xd_copy(far, k).wait_recv()
            else:
                for copy in x_copies(far, k):
                    copy.wait_recv()
            r = relay_d if down else relay
            r(far, rep, k, y_send, y_recv, over_y).start()
            r(far, rep, k, sx_send, sx_recv, over_core).start()

        relays((n - 3) // 2, forward_x)

        def arrived(k, down):
            r = relay_d if down else relay
            other = (beside + 2) % 4
            r(other, rep, k, sx_send, sx_recv, over_core).wait_recv()
            r(other, 1 - rep, k, sy_send, sy_recv, over_core).wait_recv()
            if not down:
                load(k).start()

        relays((n - 7) // 2, arrived)

    @pl.when(n % 2 == 0)
    def _():
        def forward_y(k, down):
            r = relay_d if down else relay
            r(far, 1 - rep, k, y_send, y_recv, over_y).wait_recv()
            r(far, 1 - rep, k, sy_send, sy_recv, over_core).start()

        relays((n - 6) // 2, forward_y)

    if not first:
        @pl.when(n < AHEAD)
        def _():
            out = jnp.dot(actp_ref[...], wdp_ref[...], preferred_element_type=WIDE).astype(NARROW)
            h = (h_ref[...].astype(WIDE) + out.astype(WIDE)).astype(NARROW)
            h_out[...] = h
            wide = h.astype(WIDE)
            scale = lax.rsqrt(jnp.mean(wide * wide, -1, keepdims=True) + 1e-6)
            size = h_ref.shape[0]
            a_ref[pl.ds(pl.multiple_of(n * size, size), size), :] = (wide * scale).astype(NARROW)

    @pl.when((n >= AHEAD) & (n < AHEAD + CHUNKS * TILES))
    def _():
        k, i = (n - AHEAD) // TILES, (n - AHEAD) % TILES

        @pl.when(i == 0)
        def _():
            load(k).wait()

        size = act_ref.shape[0]
        a = a_ref[pl.ds(pl.multiple_of(i * size, size), size), :]
        gate = jnp.dot(a, slots[k % 2, 0], preferred_element_type=WIDE)
        up = jnp.dot(a, slots[k % 2, 1], preferred_element_type=WIDE)
        gate_ref[...] = gate
        up_ref[...] = up
        act_ref[...] = (gate * jax.nn.sigmoid(gate) * up).astype(NARROW)

    @pl.when(n == pl.num_programs(0) - 1)
    def _():
        for copy in own_copies(dp):
            copy.wait_send()
        for k in range(CHUNKS):
            for copy in x_copies(dp, k):
                copy.wait_send()
        for k in range(PIECES):
            xd_copy(dp, k).wait_send()
        for k in range(CHUNKS):
            relay(far, rep, k, y_send, y_recv, over_y).wait_send()
            relay(far, rep, k, sx_send, sx_recv, over_core).wait_send()
            relay(far, 1 - rep, k, sy_send, sy_recv, over_core).wait_send()
        for k in range(PIECES):
            relay_d(far, rep, k, y_send, y_recv, over_y).wait_send()
            relay_d(far, rep, k, sx_send, sx_recv, over_core).wait_send()
            relay_d(far, 1 - rep, k, sy_send, sy_recv, over_core).wait_send()


def forward(number, h, before, wg, wu, wd):
    first = before is None
    tokens, d = h.shape
    rows_gu, ff = wg.shape[1:]
    rows_d = wd.shape[1]
    cols, tile, small = ff // CHUNKS, tokens // TILES, tokens // AHEAD
    steps = 2 * (CHUNKS + PIECES) + 6

    def at(n):
        m = jnp.clip(n - AHEAD, 0, CHUNKS * TILES - 1)
        return m % TILES, m // TILES

    def whole(shape):
        return pl.BlockSpec(shape, lambda n: (0, 0), pipeline_mode=pl.Buffered(1))

    def slice_of(width):
        return pl.BlockSpec((small, width), lambda n: (jnp.minimum(n, AHEAD - 1), 0))

    tiles = pl.BlockSpec((tile, cols), at)
    out_shape = [jax.ShapeDtypeStruct((tokens, ff), NARROW)] + [jax.ShapeDtypeStruct((tokens, ff), WIDE)] * 2 + [jax.ShapeDtypeStruct((tokens, d), NARROW)]
    out_specs = [tiles] * 3 + [whole((tokens, d))]
    if first:
        inputs, in_specs = [h], [whole((tokens, d))]
    else:
        inputs, in_specs = [h, *before], [slice_of(d), slice_of(ff), whole((ff, d))]
        out_shape.append(jax.ShapeDtypeStruct((tokens, d), NARROW))
        out_specs.append(slice_of(d))
    out_shape += [jax.ShapeDtypeStruct((2, 4 * rows_gu, ff), NARROW), jax.ShapeDtypeStruct((4 * rows_d, d), NARROW)]
    dma = pltpu.SemaphoreType.DMA
    both = CHUNKS + PIECES
    flops = 4 * tokens * d * ff
    return pl.pallas_call(
        functools.partial(forward_kernel, number, first),
        grid=(steps,),
        in_specs=in_specs + [WHOLE] * 3,
        out_specs=out_specs + [WHOLE] * 2,
        out_shape=out_shape,
        scratch_shapes=[
            pltpu.VMEM((2, 2, 4 * rows_gu, cols), NARROW),
            pltpu.VMEM((2, rows_gu, ff), NARROW),
            pltpu.VMEM((rows_d, d), NARROW),
            dma((6,)), dma((2,)), dma((3,)), dma((3,)),
            dma((2, CHUNKS)), dma((2, CHUNKS)), dma((PIECES,)), dma((PIECES,)),
            dma((both,)), dma((both,)), dma((both,)), dma((both,)), dma((both,)), dma((both,)),
        ],
        compiler_params=pltpu.CompilerParams(collective_id=number, has_side_effects=True, vmem_limit_bytes=63 * MIB),
        cost_estimate=pl.CostEstimate(flops=flops, bytes_accessed=100 * MIB, transcendentals=tokens * ff),
        name=f"forward_{number}",
    )(*inputs, wg, wu, wd)


def normed_back(h, by_a, by_h):
    wide, by_a = h.astype(WIDE), by_a.astype(WIDE)
    scale = lax.rsqrt(jnp.mean(wide**2, -1, keepdims=True) + 1e-6)
    by_scale = jnp.sum(by_a * wide, -1, keepdims=True)
    by_wide = by_a * scale - wide * (by_scale * scale**3 / wide.shape[-1])
    return by_h + by_wide.astype(NARROW)


def dot(a, b, over):
    return lax.dot_general(a, b, (over, ((), ())), preferred_element_type=WIDE)


def adamw(w, m, v, g):
    m = 0.9 * m + 0.1 * g
    v = 0.95 * v + 0.05 * g * g
    step = m * lax.rsqrt(v + 1e-8) + 0.1 * w
    return (w - 0.02 * step).astype(NARROW), m, v


def solution(mesh):
    def scattered(left, right):
        return lax.psum_scatter(dot(left, right, ((0,), (0,))).astype(NARROW), "dp", scatter_dimension=0, tiled=True)

    def step(x, dy, *arrays):
        weights, m, v = (arrays[i : i + 3] for i in (0, 3, 6))
        layers = weights[0].shape[0]
        h, before, kept = x[0], None, []
        for number in range(layers):
            act, gate, up, a, *rest = forward(number, h, before, *weights)
            if number:
                h, gu, down = rest
            else:
                gu, down = rest
            kept.append((h, a, gate, up, act, gu, down))
            before = act, down
        by_h, mine = dy[0], [None] * layers
        for number in reversed(range(layers)):
            h, a, gate, up, act, gu, down = kept[number]
            by_down = scattered(act, by_h)
            by_act = dot(by_h, down, ((1,), (1,))).astype(NARROW).astype(WIDE)
            sig = jax.nn.sigmoid(gate)
            by_up = (by_act * (gate * sig)).astype(NARROW)
            by_gate = (by_act * up * (sig * (1 + gate * (1 - sig)))).astype(NARROW)
            mine[number] = [scattered(a, by_gate), scattered(a, by_up), by_down]
            if number:
                by_a = dot(by_gate, gu[0], ((1,), (1,))).astype(NARROW) + dot(by_up, gu[1], ((1,), (1,))).astype(NARROW)
                by_h = normed_back(h, by_a, by_h)
        gradients = [jnp.stack([mine[number][i] for number in range(layers)]).astype(WIDE) for i in range(3)]
        new = [adamw(w.astype(WIDE), m, v, g) for w, m, v, g in zip(weights, m, v, gradients, strict=True)]
        return tuple(one[which] for which in range(3) for one in new)

    states, cut = P(("rep", "dp"), None, None), P(None, "dp", None)
    return jax.shard_map(
        step,
        mesh=mesh,
        in_specs=(states, states) + (cut,) * 9,
        out_specs=(P("rep", "dp", None),) * 9,
        check_vma=False,
    )
```

time: 1140 us -> 871 us (0.76)
  waiting for transfers between devices: 508 us -> 247 us
  Pallas kernels: 0 us -> 216 us
  matrix products: 498 us -> 318 us
  local copies, waits for them, and re-layouts: 33.3 us -> 0 us
    all_gather x6 -> x0, waiting for transfers between devices: 229 us -> none  [fetched(): lax.all_gather(w[number], 'dp', axis=0, tiled=True)]
    pallas_call x0 -> x2, Pallas kernels: none -> 216 us  [forward(): pl.pallas_call(functools.partial(forward_kernel, number, first), grid=(st...]
    dot_general x15 -> x10, matrix products: 498 us -> 318 us  [dot(): return lax.dot_general(a, b, (over, ((), ())), preferred_element_type=WIDE)]
    reduce_scatter x6, waiting for transfers between devices: 278 us -> 247 us  [scattered(): lax.psum_scatter(dot(left, right, ((0,), (0,))).astype(NARROW), 'dp', sca...]
    unnamed x16 -> x0, local copies, waits for them, and re-layouts: 17 us -> none
    slice x3 -> x0, local copies, waits for them, and re-layouts: 16.3 us -> none  [fetched(): w[number]]
    add_any x1 -> x0, other arithmetic: 12.4 us -> none  [normed(): wide = h.astype(jnp.float32)]
  transfers between devices with their start and end apart: 12 -> 6, of which waited for: 10 -> 4; matrix products, arithmetic and copies ran while one was open for 35% -> 34% of each run, Pallas kernels for 0% -> 0%
where the time goes in v1:
time: 871 us; the launch traced here: 864 us
  matrix products  318 us (37%)
  waiting for transfers between devices  247 us (28%)
  Pallas kernels  216 us (25%)
  other arithmetic  69.1 us (8%)
  between operations  14.3 us (2%)
    dot_general x10, matrix products, dot(): return lax.dot_general(a, b, (over, ((), ())), preferred_element_type=WIDE)  318 us
    reduce_scatter x6, waiting for transfers between devices, scattered(): lax.psum_scatter(dot(left, right, ((0,), (0,))).astype(NARROW), 'dp', sca...  247 us
    pallas_call x2, Pallas kernels, forward(): pl.pallas_call(functools.partial(forward_kernel, number, first), grid=(st...  216 us
    convert_element_type x3, other arithmetic, adamw(): return ((w - 0.02 * step).astype(NARROW), m, v)  59.6 us
  transfers between devices with their start and end apart: 6, of which 4 were waited for; matrix products, arithmetic and copies ran while one was open for 34% of the time, Pallas kernels for 0%

profile of v1, /device:TPU:0, one launch (start us, length us, event | category | flops | bytes accessed | tf_op | source)
XLA Modules:
  0.0 864.3 jit_solution(10265859350576068217)
XLA Ops:
  7.2 106.7 %forward_0.1 = (bf16[2048,4096]{1,0:T(8,128)(2,1)}, f32[2048,4096]{1,0:T(8,128)}, f32[2048,4096]{1,0:T(8,128)}, bf16[2048,1280]{1,0:T(8,128)(2,1)}, bf16[2,1280,...) custom-call(bf16[2048,1280]{1,0:T(8,128)(2,1)} %bitcast.58, bf16[2,320,4096]{2,1,0:T(8,128)(2,1)} %refs_3_.3, ...), custom_call_target="tpu_custom_call" | custom-call | flops 42949672960 | bytes 104857600 | tf_op jit(solution)/shard_map/forward_0/pallas_call | solution.py:240
  113.9 109.2 %forward_1.1 = (bf16[2048,4096]{1,0:T(8,128)(2,1)}, f32[2048,4096]{1,0:T(8,128)}, f32[2048,4096]{1,0:T(8,128)}, bf16[2048,1280]{1,0:T(8,128)(2,1)}, bf16[2048,12...) custom-call(bf16[2048,1280]{1,0:T(8,128)(2,1)} %bitcast.59, ...), custom_call_target="tpu_custom_call" | custom-call | flops 42949672960 | bytes 104857600 | tf_op jit(solution)/shard_map/forward_1/pallas_call | solution.py:240
  223.1 45.8 %fusion.5 = (bf16[2048,4096]{1,0:T(8,128)(2,1)}, bf16[2048,4096]{1,0:T(8,128)(2,1)}) fusion(f32[2048,4096]{1,0:T(8,128)} %get-tuple-element.26, f32[2048,4096]{1,0:T(8,128)} %get-tuple-element.25, bf16[4096,1280]{1,0:T(8,128)(2,1)} %get-tuple-element.24, bf16[1,2048,1280]{2,1,0:T(8,128)(2,1)} %param.12), kind=kOutput, calls=%fused_computation.9 | convolution fusion | flops 21600665600 | bytes 116391936 | tf_op jit(solution)/shard_map/dot_general | solution.py:269
  268.9 27.9 %convolution_convert_fusion.4 = bf16[1280,4096]{1,0:T(8,128)(2,1)} fusion(bf16[2048,1280]{1,0:T(8,128)(2,1)} %get-tuple-element.31, bf16[2048,4096]{1,0:T(8,128)(2,1)} %get-tuple-element.45), kind=kOutput, calls=%fused_computation.26 | convolution fusion | flops 21480079360 | bytes 32505856 | tf_op jit(solution)/shard_map/dot_general | solution.py:269
  296.9 0.0 reduce-scatter.7.cloned.1.call-start
  296.9 29.0 %fusion.41 = bf16[2048,1280]{1,0:T(8,128)(2,1)} fusion(bf16[2048,4096]{1,0:T(8,128)(2,1)} %get-tuple-element.45, bf16[2,1280,4096]{2,1,0:T(8,128)(2,1)} %get-tuple-element.27), kind=kOutput, calls=%fused_computation.63 | convolution fusion | flops 21477457920 | bytes 32505856 | tf_op jit(solution)/shard_map/dot_general | solution.py:269
  325.9 30.6 %fusion.30 = (f32[2048]{0:T(1024)S(1)}, f32[2048]{0:T(1024)S(1)}, bf16[2048,1280]{1,0:T(8,128)(2,1)}) fusion(bf16[2048,1280]{1,0:T(8,128)(2,1)} %get-tuple-element.28, bf16[2048,1280]{1,0:T(8,128)(2,1)} %fusion.41, bf16[2048,4096]{1,0:T(8,128)(2,1)} %get-tuple-element.44, bf16[2,1280,4096]{2,1,0:T(8,128)(2,1)} %get-tuple-element.27), kind=kOutput, calls=%fused_computation.52 | convolution fusion | flops 21495803904 | bytes 43008000 | tf_op jit(solution)/shard_map/dot_general | solution.py:269
  356.5 9.5 %fusion.50 = bf16[2048,1280]{1,0:T(8,128)(2,1)} fusion(bf16[2048,1280]{1,0:T(8,128)(2,1)} %get-tuple-element.28, bf16[2048,1280]{1,0:T(8,128)(2,1)} %get-tuple-element.48, bf16[1,2048,1280]{2,1,0:T(8,128)(2,1)} %param.12, f32[2048]{0:T(1024)S(1)} %get-tuple-element.47, f32[2048]{0:T(1024)S(1)} %get-tuple-element.46), kind=kLoop, calls=%fused_computation.66 | loop fusion | flops 18350080 | bytes 20987904 | tf_op jit(solution)/shard_map/add | solution.py:265
  366.0 29.1 %convolution_convert_fusion.5 = bf16[2048,4096]{1,0:T(8,128)(2,1)} fusion(bf16[2048,1280]{1,0:T(8,128)(2,1)} %fusion.50, bf16[4096,1280]{1,0:T(8,128)(2,1)} %get-tuple-element.23.refs_2_), kind=kOutput, calls=%fused_computation.27 | convolution fusion | flops 21483225088 | bytes 32505856 | tf_op jit(solution)/shard_map/dot_general | solution.py:269
  395.1 39.8 %fusion.10 = bf16[1280,4096]{1,0:T(8,128)(2,1)} fusion(bf16[2048,1280]{1,0:T(8,128)(2,1)} %get-tuple-element.21, f32[2048,4096]{1,0:T(8,128)} %get-tuple-element.29, bf16[2048,4096]{1,0:T(8,128)(2,1)} %convolution_convert_fusion.5, f32[2048,4096]{1,0:T(8,128)} %get-tuple-element.30), kind=kOutput, calls=%fused_computation.20 | convolution fusion | flops 21572354048 | bytes 99614720 | tf_op jit(solution)/shard_map/dot_general | solution.py:269
  434.9 0.0 reduce-scatter.13.cloned.1.call-start
  435.0 28.4 %convolution_convert_fusion.3 = bf16[1280,4096]{1,0:T(8,128)(2,1)} fusion(bf16[2048,1280]{1,0:T(8,128)(2,1)} %get-tuple-element.31, bf16[2048,4096]{1,0:T(8,128)(2,1)} %get-tuple-element.44), kind=kOutput, calls=%fused_computation.25 | convolution fusion | flops 21480079360 | bytes 32505856 | tf_op jit(solution)/shard_map/dot_general | solution.py:269
  463.4 0.0 reduce-scatter.11.cloned.1.call-start
  463.4 30.8 %fusion.13 = bf16[1280,4096]{1,0:T(8,128)(2,1)} fusion(bf16[2048,1280]{1,0:T(8,128)(2,1)} %get-tuple-element.21, bf16[2048,4096]{1,0:T(8,128)(2,1)} %convolution_convert_fusion.5, f32[2048,4096]{1,0:T(8,128)} %get-tuple-element.30), kind=kOutput, calls=%fused_computation.21 | convolution fusion | flops 21538799616 | bytes 66060288 | tf_op jit(solution)/shard_map/dot_general | solution.py:269
  494.3 28.5 %convolution_convert_fusion.2 = bf16[4096,1280]{1,0:T(8,128)(2,1)} fusion(bf16[2048,4096]{1,0:T(8,128)(2,1)} %get-tuple-element.22.refs_1_, bf16[2048,1280]{1,0:T(8,128)(2,1)} %fusion.50), kind=kOutput, calls=%fused_computation.24 | convolution fusion | flops 21480079360 | bytes 32505856 | tf_op jit(solution)/shard_map/dot_general | solution.py:269
  522.8 0.0 reduce-scatter.17.cloned.1.call-start
  522.9 28.2 %convolution_convert_fusion.1 = bf16[4096,1280]{1,0:T(8,128)(2,1)} fusion(bf16[2048,4096]{1,0:T(8,128)(2,1)} %get-tuple-element.32, bf16[1,2048,1280]{2,1,0:T(8,128)(2,1)} %param.12), kind=kOutput, calls=%fused_computation.23 | convolution fusion | flops 21480079360 | bytes 32505856 | tf_op jit(solution)/shard_map/dot_general | solution.py:269
  551.1 19.0 %fusion.18 = (bf16[2,320,4096]{2,1,0:T(8,128)(2,1)}, f32[2,320,4096]{2,1,0:T(8,128)}, f32[2,320,4096]{2,1,0:T(8,128)}) fusion(bf16[2,320,4096]{2,1,0:T(8,128)(2,1)} %refs_3_.3, bf16[1,320,4096]{2,1,0:T(8,128)(2,1)} %bitcast.52, bf16[1,320,4096]{2,1,0:T(8,128)(2,1)} %bitcast.53, f32[2,320,4096]{2,1,0:T(8,128)} %param.19, f32[2,320,4096]{2,1,0:T(8,128)} %param.16), kind=kLoop, calls=%fused_computation.40 | loop fusion | flops 49807360 | bytes 57671680 | tf_op jit(solution)/shard_map/convert_element_type | solution.py:276
  570.1 23.9 %reduce-scatter.13.cloned.1.call-done = bf16[320,4096]{1,0:T(8,128)(2,1)} async-done(((bf16[1280,4096]{1,0:T(8,128)(2,1)}), bf16[320,4096]{1,0:T(8,128)(2,1)}) %reduce-scatter.13.cloned.1.call-update) | async-done | bytes 2621456 | tf_op jit(solution)/shard_map/reduce_scatter | solution.py:281
  594.1 80.9 %reduce-scatter.11.cloned.1.call-done = bf16[320,4096]{1,0:T(8,128)(2,1)} async-done(((bf16[1280,4096]{1,0:T(8,128)(2,1)}), bf16[320,4096]{1,0:T(8,128)(2,1)}) %reduce-scatter.11.cloned.1.call-update) | async-done | bytes 2621456 | tf_op jit(solution)/shard_map/reduce_scatter | solution.py:281
  675.0 19.0 %fusion.24 = (bf16[2,320,4096]{2,1,0:T(8,128)(2,1)}, f32[2,320,4096]{2,1,0:T(8,128)}, f32[2,320,4096]{2,1,0:T(8,128)}) fusion(bf16[2,320,4096]{2,1,0:T(8,128)(2,1)} %refs_4_.1, bf16[1,320,4096]{2,1,0:T(8,128)(2,1)} %bitcast.54, bf16[1,320,4096]{2,1,0:T(8,128)(2,1)} %bitcast.55, f32[2,320,4096]{2,1,0:T(8,128)} %param.20, f32[2,320,4096]{2,1,0:T(8,128)} %param.17), kind=kLoop, calls=%fused_computation.46 | loop fusion | flops 49807360 | bytes 57671680 | tf_op jit(solution)/shard_map/convert_element_type | solution.py:276
  693.9 61.4 %reduce-scatter.15.cloned.1.call-done = bf16[1024,1280]{1,0:T(8,128)(2,1)} async-done(((bf16[4096,1280]{1,0:T(8,128)(2,1)}), bf16[1024,1280]{1,0:T(8,128)(2,1)}) %reduce-scatter.15.cloned.1.call-update) | async-done | bytes 2621456 | tf_op jit(solution)/shard_map/reduce_scatter | solution.py:281
  755.3 80.3 %reduce-scatter.17.cloned.1.call-done = bf16[1024,1280]{1,0:T(8,128)(2,1)} async-done(((bf16[4096,1280]{1,0:T(8,128)(2,1)}), bf16[1024,1280]{1,0:T(8,128)(2,1)}) %reduce-scatter.17.cloned.1.call-update) | async-done | bytes 2621456 | tf_op jit(solution)/shard_map/reduce_scatter | solution.py:281
  835.6 21.7 %fusion.28 = (bf16[2,1024,1280]{2,1,0:T(8,128)(2,1)}, f32[2,1024,1280]{2,1,0:T(8,128)}, f32[2,1024,1280]{2,1,0:T(8,128)}) fusion(bf16[2,1024,1280]{2,1,0:T(8,128)(2,1)} %refs_5_.1, bf16[1,1024,1280]{2,1,0:T(8,128)(2,1)} %bitcast.57, bf16[1,1024,1280]{2,1,0:T(8,128)(2,1)} %bitcast.56, f32[2,1024,1280]{2,1,0:T(8,128)} %param.21, f32[2,1024,1280]{2,1,0:T(8,128)} %param.18), kind=kLoop, calls=%fused_computation.50 | loop fusion | flops 49807360 | bytes 57671680 | tf_op jit(solution)/shard_map/convert_element_type | solution.py:276
  (11 shorter events, 0.2 us)
Async XLA Ops:
  7.2 543.9 %reduce-scatter.9.cloned.1.call-start = ((), (), s32[]{:S(2)}) async-start(), calls=%async_computation.7 | async-start | bytes 13107200 | tf_op jit(solution)/shard_map/reduce_scatter | solution.py:281
  296.9 254.3 %reduce-scatter.7.cloned.1.call-start = ((), (), s32[]{:S(2)}) async-start(), calls=%async_computation.6 | async-start | bytes 13107200 | tf_op jit(solution)/shard_map/reduce_scatter | solution.py:281
  434.9 159.1 %reduce-scatter.13.cloned.1.call-start = ((), (), s32[]{:S(2)}) async-start(), calls=%async_computation.9 | async-start | bytes 13107200 | tf_op jit(solution)/shard_map/reduce_scatter | solution.py:281
  463.4 211.6 %reduce-scatter.11.cloned.1.call-start = ((), (), s32[]{:S(2)}) async-start(), calls=%async_computation.8 | async-start | bytes 13107200 | tf_op jit(solution)/shard_map/reduce_scatter | solution.py:281
  494.3 261.0 %reduce-scatter.15.cloned.1.call-start = ((), (), s32[]{:S(2)}) async-start(), calls=%async_computation.10 | async-start | bytes 13107200 | tf_op jit(solution)/shard_map/reduce_scatter | solution.py:281
  522.8 312.7 %reduce-scatter.17.cloned.1.call-start = ((), (), s32[]{:S(2)}) async-start(), calls=%async_computation.11 | async-start | bytes 13107200 | tf_op jit(solution)/shard_map/reduce_scatter | solution.py:281
Sparse Core Ops, SparseCore 0:
  297.0 77.9 reduce-scatter.8
  435.0 77.9 reduce-scatter.6
  516.1 77.8 reduce-scatter.12
  597.0 77.8 reduce-scatter.10
  677.4 77.8 reduce-scatter.14
  757.7 77.8 reduce-scatter.16
